TPU v7x, 32 devices: a whole 2x2x4 slice. The times are simulated.
32 devices in a mesh: dp: 4 (over y, x), expert: 8 (over z, core).
Axes of the slice: x: 2, y: 2, z: 4, core: 2. Of those that a mesh axis runs over, the one named last changes fastest.
Arguments:
- tokens: bfloat16 [4096, 2048], P(('dp', 'expert')), may hold values from -6 to 6
- expert_ids: int32 [4096, 2], P(('dp', 'expert')), may hold values from 0 to 7, all different within a row; in each aligned block of 128 rows (0 to 127, 128 to 255, ...) at most 48 rows name the same one
- route_weights: float32 [4096, 2], P(('dp', 'expert')), may hold values from 0.1 to 1
- w_gate: bfloat16 [8, 2048, 384], P('expert', 'dp'), may hold values from -0.125 to 0.125
- w_up: bfloat16 [8, 2048, 384], P('expert', 'dp'), may hold values from -0.125 to 0.125
- w_down: bfloat16 [8, 2048, 384], P('expert', 'dp'), may hold values from -0.3125 to 0.3125
- grad_out: bfloat16 [4096, 2048], P(('dp', 'expert')), may hold values from -6 to 6
Outputs:
- layer_out: bfloat16 [4096, 2048], P(('dp', 'expert'))
- token_grad: bfloat16 [4096, 2048], P(('dp', 'expert'))
- route_grad: float32 [4096, 2], P(('dp', 'expert'))
- gate_grad: bfloat16 [8, 2048, 384], P('expert', 'dp')
- up_grad: bfloat16 [8, 2048, 384], P('expert', 'dp')
- down_grad: bfloat16 [8, 2048, 384], P('expert', 'dp')
Inputs may be any that keep to these rules, and one draw needn't show every extreme that they name: `expert_ids`: each token names 2 different experts. Among the tokens of one device (aligned blocks of 128 tokens) no expert is named more than 48 times, and in some blocks one is named exactly 48 times.
All inputs are finite; a program needn't handle non-finite values.
Results may differ from a plain program's by a relative error of at most 0.0065.
Values may be sent and summed in bfloat16 or wider, within the bound.
A program may use at most 64 MiB of HBM per device.

v0:
```python
import jax
import jax.numpy as jnp
from jax import lax
from jax.sharding import PartitionSpec as P


def slot_table(expert_ids, experts, capacity):
    flat = expert_ids.reshape(-1)
    count = flat.shape[0]
    same = flat[:, None] == flat[None, :]
    earlier = lax.broadcasted_iota(jnp.int32, (count, count), 0) > lax.broadcasted_iota(
        jnp.int32, (count, count), 1
    )
    rank = jnp.sum((same & earlier).astype(jnp.int32), axis=1)
    target = flat * capacity + rank
    columns = lax.broadcasted_iota(jnp.int32, (count, experts * capacity), 1)
    return (target[:, None] == columns).astype(jnp.bfloat16)


def contract_last(left, right):
    return lax.dot_general(
        left, right, (((1,), (1,)), ((), ())), preferred_element_type=jnp.float32
    )


def contract_first(left, right):
    return lax.dot_general(
        left, right, (((0,), (0,)), ((), ())), preferred_element_type=jnp.float32
    )


def expert_forward(rows, gate_w, up_w, down_w):
    gate = jnp.dot(rows, gate_w, preferred_element_type=jnp.float32)
    up = jnp.dot(rows, up_w, preferred_element_type=jnp.float32)
    sig = jax.nn.sigmoid(gate)
    hidden = (gate * sig * up).astype(jnp.bfloat16)
    expert_out = contract_last(hidden, down_w).astype(jnp.bfloat16)
    return (expert_out, (gate, up, sig, hidden))


def expert_backward(out_grad, saved, gate_w, up_w, down_w):
    gate, up, sig, hidden = saved
    hidden_grad = jnp.dot(out_grad, down_w, preferred_element_type=jnp.float32)
    gate_term = (hidden_grad * up * sig * (1.0 + gate * (1.0 - sig))).astype(jnp.bfloat16)
    up_term = (hidden_grad * gate * sig).astype(jnp.bfloat16)
    slot_grad = (contract_last(gate_term, gate_w) + contract_last(up_term, up_w)).astype(
        jnp.bfloat16
    )
    return (slot_grad, gate_term, up_term)


def weight_grads(rows, out_grad, gate_term, up_term, hidden):
    part_rows, part_grad = (
        lax.all_to_all(rows, "dp", split_axis=1, concat_axis=0, tiled=True),
        lax.all_to_all(out_grad, "dp", split_axis=1, concat_axis=0, tiled=True),
    )
    all_gate, all_up, all_hidden = (
        lax.all_gather(gate_term, "dp", axis=0, tiled=True),
        lax.all_gather(up_term, "dp", axis=0, tiled=True),
        lax.all_gather(hidden, "dp", axis=0, tiled=True),
    )
    down_g = contract_first(part_grad, all_hidden).astype(jnp.bfloat16)
    gate_g = contract_first(part_rows, all_gate).astype(jnp.bfloat16)
    up_g = contract_first(part_rows, all_up).astype(jnp.bfloat16)
    return (gate_g, up_g, down_g)


def body(tokens, expert_ids, route_weights, w_gate, w_up, w_down, grad_out):
    local = w_gate.shape[0]
    groups = lax.axis_size("expert")
    experts = local * groups
    count = tokens.shape[0]
    top = expert_ids.shape[1]
    width = tokens.shape[1]
    capacity = max(2, (3 * count * top + 2 * experts - 1) // (2 * experts))
    table = slot_table(expert_ids, experts, capacity)
    per_token = jnp.sum(table.reshape(count, top, experts * capacity), axis=1)
    send_rows = jnp.dot(per_token.T, tokens, preferred_element_type=jnp.float32)
    send_rows = send_rows.astype(jnp.bfloat16).reshape(experts, capacity, width)
    weighted = (route_weights[:, :, None] * grad_out.astype(jnp.float32)[:, None, :]).astype(
        jnp.bfloat16
    )
    send_grad = jnp.dot(
        table.T, weighted.reshape(count * top, width), preferred_element_type=jnp.float32
    )
    send_grad = send_grad.astype(jnp.bfloat16).reshape(experts, capacity, width)
    full_gate, full_up, full_down = (
        lax.all_gather(w_gate, "dp", axis=1, tiled=True),
        lax.all_gather(w_up, "dp", axis=1, tiled=True),
        lax.all_gather(w_down, "dp", axis=1, tiled=True),
    )
    received = lax.all_to_all(send_rows, "expert", split_axis=0, concat_axis=0, tiled=True)
    shaped = received.reshape(groups, local, capacity, width)
    saves = []
    inputs = []
    slot_expert = 0
    rows = shaped[:, slot_expert].reshape(groups * capacity, width)
    expert_out, saved = expert_forward(
        rows, full_gate[slot_expert], full_up[slot_expert], full_down[slot_expert]
    )
    outs = expert_out.reshape(groups, 1, capacity, width)
    saves.append(saved)
    inputs.append(rows)
    expert_outs, saves, inputs = (outs.reshape(experts, capacity, width), saves, inputs)
    back_out = lax.all_to_all(expert_outs, "expert", split_axis=0, concat_axis=0, tiled=True)
    received_grad = lax.all_to_all(send_grad, "expert", split_axis=0, concat_axis=0, tiled=True)
    shaped = received_grad.reshape(groups, local, capacity, width)
    slot_expert = 0
    out_grad = shaped[:, slot_expert].reshape(groups * capacity, width)
    slot_grad, gate_term, up_term = expert_backward(
        out_grad,
        saves[slot_expert],
        full_gate[slot_expert],
        full_up[slot_expert],
        full_down[slot_expert],
    )
    grads_in = slot_grad.reshape(groups, 1, capacity, width)
    gate_g, up_g, down_g = weight_grads(
        inputs[slot_expert], out_grad, gate_term, up_term, saves[slot_expert][3]
    )
    gate_list = [gate_g]
    up_list = [up_g]
    down_list = [down_g]
    slot_grads = grads_in.reshape(experts, capacity, width)
    gate_grad = jnp.stack(gate_list)
    up_grad = jnp.stack(up_list)
    down_grad = jnp.stack(down_list)
    back_grad = lax.all_to_all(slot_grads, "expert", split_axis=0, concat_axis=0, tiled=True)
    out_slots = jnp.dot(
        table, back_out.reshape(experts * capacity, width), preferred_element_type=jnp.float32
    )
    out_slots = out_slots.reshape(count, top, width)
    layer_out = jnp.sum(route_weights[:, :, None] * out_slots, axis=1).astype(jnp.bfloat16)
    route_grad = jnp.sum(grad_out.astype(jnp.float32)[:, None, :] * out_slots, axis=2)
    grad_slots = jnp.dot(
        table, back_grad.reshape(experts * capacity, width), preferred_element_type=jnp.float32
    )
    token_grad = jnp.sum(grad_slots.reshape(count, top, width), axis=1).astype(jnp.bfloat16)
    return (layer_out, token_grad, route_grad, gate_grad, up_grad, down_grad)


def solution(mesh):
    in_specs = (
        P(("dp", "expert"), None),
        P(("dp", "expert"), None),
        P(("dp", "expert"), None),
        P("expert", "dp", None),
        P("expert", "dp", None),
        P("expert", "dp", None),
        P(("dp", "expert"), None),
    )
    out_specs = (
        P(("dp", "expert"), None),
        P(("dp", "expert"), None),
        P(("dp", "expert"), None),
        P("expert", "dp", None),
        P("expert", "dp", None),
        P("expert", "dp", None),
    )
    return jax.shard_map(body, mesh=mesh, in_specs=in_specs, out_specs=out_specs, check_vma=False)
```

profile of v0, /device:TPU:0, one launch (start us, length us, event | category | flops | bytes accessed | tf_op | source)
XLA Modules:
  0.0 245.1 jit_solution(16836155840150833986)
XLA Ops:
  10.1 1.7 convolution_convert_fusion.2
  11.8 6.5 %all-to-all-start = ((bf16[8,48,2048]{2,1,0:T(8,128)(2,1)}), bf16[8,48,2048]{2,1,0:T(8,128)(2,1)}, u32[]{:S(2)}, u32[]{:S(2)}) async-start(bf16[8,48,2048]{2,1,0:T(8,128)(2,1)} %bitcast.1), calls=%async_computation | async-start | bytes 3145728 | tf_op jit(solution)/shard_map/all_to_all | solution.py:92
  20.1 2.4 mul.82
  22.8 3.4 %convolution_convert_fusion.1 = bf16[384,2048]{1,0:T(8,128)(2,1)} fusion(f32[256,2048]{1,0:T(8,128)} %mul.82, f32[256]{0:T(256)S(1)} %mul.79, s32[256]{0:T(256)S(1)} %multiply_add_fusion), kind=kOutput, calls=%fused_computation.2 | convolution fusion | flops 404586496 | bytes 3672064 | tf_op jit(solution)/shard_map/dot_general | solution.py:83
  26.3 29.9 %all-to-all-done = bf16[8,48,2048]{2,1,0:T(8,128)(2,1)} async-done(((bf16[8,48,2048]{2,1,0:T(8,128)(2,1)}), bf16[8,48,2048]{2,1,0:T(8,128)(2,1)}, u32[]{:S(2)}, u32[]{:S(2)}) %all-to-all-start) | async-done | bytes 1572896 | tf_op jit(solution)/shard_map/all_to_all | solution.py:92
  56.2 3.6 %all-to-all-start.2 = ((bf16[8,48,2048]{2,1,0:T(8,128)(2,1)}), bf16[8,48,2048]{2,1,0:T(8,128)(2,1)S(1)}, u32[]{:S(2)}, u32[]{:S(2)}) async-start(bf16[8,48,2048]{2,1,0:T(8,128)(2,1)} %bitcast.64), calls=%async_computation.2 | async-start | bytes 3145728 | tf_op jit(solution)/shard_map/all_to_all | solution.py:106
  60.5 3.8 %all_to_all.44 = bf16[384,4,512]{2,1,0:T(4,128)(2,1)} reshape(bf16[8,48,2048]{2,1,0:T(8,128)(2,1)} %all-to-all-done) | data formatting | bytes 3145728 | tf_op jit(solution)/shard_map/all_to_all | solution.py:54
  64.4 3.1 %copy.49 = bf16[384,4,512]{2,0,1:T(8,128)(2,1)} copy(bf16[384,4,512]{2,1,0:T(4,128)(2,1)} %all_to_all.44) | data formatting | bytes 3145728 | tf_op jit(solution)/shard_map/all_to_all | solution.py:54
  67.4 30.1 %all-to-all-done.2 = bf16[8,48,2048]{2,1,0:T(8,128)(2,1)S(1)} async-done(((bf16[8,48,2048]{2,1,0:T(8,128)(2,1)}), bf16[8,48,2048]{2,1,0:T(8,128)(2,1)S(1)}, u32[]{:S(2)}, u32[]{:S(2)}) %all-to-all-start.2) | async-done | bytes 1572896 | tf_op jit(solution)/shard_map/all_to_all | solution.py:106
  97.5 4.3 %all-to-all-start.4 = ((bf16[384,4,512]{2,0,1:T(8,128)(2,1)}), bf16[384,4,512]{2,0,1:T(8,128)(2,1)}, u32[]{:S(2)}, u32[]{:S(2)}) async-start(bf16[384,4,512]{2,0,1:T(8,128)(2,1)} %copy.49), calls=%async_computation.4 | async-start | bytes 3145728 | tf_op jit(solution)/shard_map/all_to_all | solution.py:54
  101.8 2.4 all_to_all.48
  104.2 2.9 %copy.50 = bf16[384,4,512]{2,0,1:T(8,128)(2,1)} copy(bf16[384,4,512]{2,1,0:T(4,128)(2,1)} %all_to_all.48) | data formatting | bytes 3145728 | tf_op jit(solution)/shard_map/all_to_all | solution.py:55
  107.1 3.7 %fusion.8 = f32[384,384]{1,0:T(8,128)} fusion(bf16[384,2048]{1,0:T(8,128)(2,1)} %bitcast.2, bf16[1,2048,384]{2,1,0:T(8,128)(2,1)} %all-gather.7.cloned.1.call-done), kind=kOutput, calls=%fused_computation.15 | convolution fusion | flops 603979776 | bytes 3735552 | tf_op jit(solution)/shard_map/dot_general | solution.py:33
  110.8 14.7 %all-to-all-done.4 = bf16[384,4,512]{2,0,1:T(8,128)(2,1)} async-done(((bf16[384,4,512]{2,0,1:T(8,128)(2,1)}), bf16[384,4,512]{2,0,1:T(8,128)(2,1)}, u32[]{:S(2)}, u32[]{:S(2)}) %all-to-all-start.4) | async-done | bytes 1572896 | tf_op jit(solution)/shard_map/all_to_all | solution.py:54
  125.5 4.4 %all-to-all-start.5 = ((bf16[384,4,512]{2,0,1:T(8,128)(2,1)}), bf16[384,4,512]{2,0,1:T(8,128)(2,1)}, u32[]{:S(2)}, u32[]{:S(2)}) async-start(bf16[384,4,512]{2,0,1:T(8,128)(2,1)} %copy.50), calls=%async_computation.5 | async-start | bytes 3145728 | tf_op jit(solution)/shard_map/all_to_all | solution.py:55
  130.0 3.7 %fusion.4 = f32[384,384]{1,0:T(8,128)} fusion(bf16[384,2048]{1,0:T(8,128)(2,1)} %bitcast.2, bf16[1,2048,384]{2,1,0:T(8,128)(2,1)} %all-gather.9.cloned.1.call-done), kind=kOutput, calls=%fused_computation.11 | convolution fusion | flops 603979776 | bytes 3735552 | tf_op jit(solution)/shard_map/dot_general | solution.py:34
  133.7 3.6 %multiply_convert_fusion.2 = (bf16[384,384]{1,0:T(8,128)(2,1)S(1)}, bf16[384,384]{1,0:T(8,128)(2,1)}, bf16[384,384]{1,0:T(8,128)(2,1)S(1)}) fusion(f32[384,384]{1,0:T(8,128)} %fusion.8, f32[384,384]{1,0:T(8,128)} %fusion.4, bf16[384,2048]{1,0:T(8,128)(2,1)S(1)} %bitcast.63, bf16[1,2048,384]{2,1,0:T(8,128)(2,1)} %all-gather.11.cloned.1.call-done), kind=kOutput, calls=%fused_computation.25 | convolution fusion | flops 606339072 | bytes 5210112 | tf_op jit(solution)/shard_map/dot_general | solution.py:43
  137.3 4.4 %fusion.6 = f32[384,2048]{1,0:T(8,128)} fusion(bf16[384,384]{1,0:T(8,128)(2,1)} %get-tuple-element.9, bf16[1,2048,384]{2,1,0:T(8,128)(2,1)} %all-gather.7.cloned.1.call-done), kind=kOutput, calls=%fused_computation.13 | convolution fusion | flops 603979776 | bytes 5013504 | tf_op jit(solution)/shard_map/dot_general | solution.py:21
  141.6 4.1 %add_convert_fusion = bf16[384,2048]{1,0:T(8,128)(2,1)} fusion(f32[384,2048]{1,0:T(8,128)} %fusion.6, bf16[384,384]{1,0:T(8,128)(2,1)S(1)} %get-tuple-element.8, bf16[1,2048,384]{2,1,0:T(8,128)(2,1)S(1)} %copy-done.2), kind=kOutput, calls=%fused_computation | convolution fusion | flops 605552640 | bytes 6586368 | tf_op jit(solution)/shard_map/dot_general | solution.py:21
  145.8 4.3 %all-to-all-done.5 = bf16[384,4,512]{2,0,1:T(8,128)(2,1)} async-done(((bf16[384,4,512]{2,0,1:T(8,128)(2,1)}), bf16[384,4,512]{2,0,1:T(8,128)(2,1)}, u32[]{:S(2)}, u32[]{:S(2)}) %all-to-all-start.5) | async-done | bytes 1572896 | tf_op jit(solution)/shard_map/all_to_all | solution.py:55
  150.1 5.0 %all-to-all-start.3 = ((bf16[8,48,2048]{2,1,0:T(8,128)(2,1)}), bf16[8,48,2048]{2,1,0:T(8,128)(2,1)S(1)}, u32[]{:S(2)}, u32[]{:S(2)}) async-start(bf16[8,48,2048]{2,1,0:T(8,128)(2,1)} %bitcast.11), calls=%async_computation.3 | async-start | bytes 3145728 | tf_op jit(solution)/shard_map/all_to_all | solution.py:128
  155.7 3.6 %convolution_convert_fusion = bf16[384,2048]{1,0:T(8,128)(2,1)} fusion(bf16[384,384]{1,0:T(8,128)(2,1)S(1)} %get-tuple-element.10, bf16[1,2048,384]{2,1,0:T(8,128)(2,1)} %all-gather.11.cloned.1.call-done), kind=kOutput, calls=%fused_computation.1 | convolution fusion | flops 604766208 | bytes 3440640 | tf_op jit(solution)/shard_map/dot_general | solution.py:21
  159.3 33.6 %all-to-all-done.3 = bf16[8,48,2048]{2,1,0:T(8,128)(2,1)S(1)} async-done(((bf16[8,48,2048]{2,1,0:T(8,128)(2,1)}), bf16[8,48,2048]{2,1,0:T(8,128)(2,1)S(1)}, u32[]{:S(2)}, u32[]{:S(2)}) %all-to-all-start.3) | async-done | bytes 1572896 | tf_op jit(solution)/shard_map/all_to_all | solution.py:128
  192.9 4.3 %all-to-all-start.1 = ((bf16[8,48,2048]{2,1,0:T(8,128)(2,1)}), bf16[8,48,2048]{2,1,0:T(8,128)(2,1)}, u32[]{:S(2)}, u32[]{:S(2)}) async-start(bf16[8,48,2048]{2,1,0:T(8,128)(2,1)} %bitcast.6), calls=%async_computation.1 | async-start | bytes 3145728 | tf_op jit(solution)/shard_map/all_to_all | solution.py:105
  197.8 1.2 convert_element_type.59
  198.9 3.5 %fusion.10 = bf16[1,512,384]{2,1,0:T(8,128)(2,1)} fusion(bf16[1536,512]{1,0:T(8,128)(2,1)} %bitcast.15, bf16[1536,384]{1,0:T(8,128)(2,1)} %all-gather.13.cloned.1.call-done), kind=kOutput, calls=%fused_computation.21 | convolution fusion | flops 604176384 | bytes 3145728 | tf_op jit(solution)/shard_map/dot_general | solution.py:27
  202.4 3.5 %fusion.11 = bf16[1,512,384]{2,1,0:T(8,128)(2,1)} fusion(bf16[1536,512]{1,0:T(8,128)(2,1)} %bitcast.15, bf16[1536,384]{1,0:T(8,128)(2,1)} %all-gather.15.cloned.1.call-done), kind=kOutput, calls=%fused_computation.22 | convolution fusion | flops 604176384 | bytes 3145728 | tf_op jit(solution)/shard_map/dot_general | solution.py:27
  206.0 22.1 %all-gather.17.cloned.1.call-done = bf16[1536,384]{1,0:T(8,128)(2,1)} async-done(((bf16[384,384]{1,0:T(8,128)(2,1)}), bf16[1536,384]{1,0:T(8,128)(2,1)}) %all-gather.17.cloned.1.call-update) | async-done | bytes 1179664 | tf_op jit(solution)/shard_map/all_gather | solution.py:60
  228.1 3.5 %fusion.12 = bf16[1,512,384]{2,1,0:T(8,128)(2,1)} fusion(bf16[1536,512]{1,0:T(8,128)(2,1)} %bitcast.20, bf16[1536,384]{1,0:T(8,128)(2,1)} %all-gather.17.cloned.1.call-done), kind=kOutput, calls=%fused_computation.23 | convolution fusion | flops 604176384 | bytes 3145728 | tf_op jit(solution)/shard_map/dot_general | solution.py:27
  231.6 1.6 convolution_reduce_fusion
  233.2 1.8 all-to-all-done.1
  235.0 3.3 %multiply_reduce_fusion = (f32[128,2]{0,1:T(2,128)}, bf16[128,2048]{1,0:T(8,128)(2,1)}) fusion(f32[128,2048]{1,0:T(8,128)S(1)} %copy-done.5, f32[128,2]{0,1:T(2,128)S(1)} %copy-done.6, bf16[384,2048,1]{1,0,2:T(8,128)(2,1)} %bitcast.8, s32[128,2]{0,1:T(2,128)S(1)} %multiply_add_fusion.1), kind=kOutput, calls=%fused_computation.4 | convolution fusion | flops 404586240 | bytes 3148800 | tf_op jit(solution)/shard_map/dot_general | solution.py:129
  (42 shorter events, 6.8 us)
Async XLA Ops:
  7.2 2.9 %copy-start = (bf16[128,2048]{1,0:T(8,128)(2,1)S(1)}, bf16[128,2048]{1,0:T(8,128)(2,1)}, u32[]{:S(2)}) copy-start(bf16[128,2048]{1,0:T(8,128)(2,1)} %param.7) | copy-start | bytes 1572868
  7.2 99.9 %all-gather.7.cloned.1.call-start = ((), (), s32[]{:S(2)}) async-start(), calls=%async_computation.6 | async-start | bytes 1966080 | tf_op jit(solution)/shard_map/all_gather | solution.py:88
  11.8 7.2 %copy-start.1 = (bf16[128,2048]{1,0:T(8,128)(2,1)S(1)}, bf16[128,2048]{1,0:T(8,128)(2,1)}, u32[]{:S(2)}) copy-start(bf16[128,2048]{1,0:T(8,128)(2,1)} %param.13) | copy-start | bytes 1572868
  11.8 44.4 %all-to-all-start = ((bf16[8,48,2048]{2,1,0:T(8,128)(2,1)}), bf16[8,48,2048]{2,1,0:T(8,128)(2,1)}, u32[]{:S(2)}, u32[]{:S(2)}) async-start(bf16[8,48,2048]{2,1,0:T(8,128)(2,1)} %bitcast.1), calls=%async_computation | async-start | bytes 3145728 | tf_op jit(solution)/shard_map/all_to_all | solution.py:92
  18.3 111.7 %all-gather.9.cloned.1.call-start = ((), (), s32[]{:S(2)}) async-start(), calls=%async_computation.7 | async-start | bytes 1966080 | tf_op jit(solution)/shard_map/all_gather | solution.py:89
  20.1 2.5 %copy-start.6 = (f32[128,2]{0,1:T(2,128)S(1)}, f32[128,2]{0,1:T(2,128)}, u32[]{:S(2)}) copy-start(f32[128,2]{0,1:T(2,128)} %param.9) | copy-start | bytes 3076
  56.2 41.3 %all-to-all-start.2 = ((bf16[8,48,2048]{2,1,0:T(8,128)(2,1)}), bf16[8,48,2048]{2,1,0:T(8,128)(2,1)S(1)}, u32[]{:S(2)}, u32[]{:S(2)}) async-start(bf16[8,48,2048]{2,1,0:T(8,128)(2,1)} %bitcast.64), calls=%async_computation.2 | async-start | bytes 3145728 | tf_op jit(solution)/shard_map/all_to_all | solution.py:106
  59.8 73.9 %all-gather.11.cloned.1.call-start = ((), (), s32[]{:S(2)}) async-start(), calls=%async_computation.8 | async-start | bytes 1966080 | tf_op jit(solution)/shard_map/all_gather | solution.py:90
  97.5 28.0 %all-to-all-start.4 = ((bf16[384,4,512]{2,0,1:T(8,128)(2,1)}), bf16[384,4,512]{2,0,1:T(8,128)(2,1)}, u32[]{:S(2)}, u32[]{:S(2)}) async-start(bf16[384,4,512]{2,0,1:T(8,128)(2,1)} %copy.49), calls=%async_computation.4 | async-start | bytes 3145728 | tf_op jit(solution)/shard_map/all_to_all | solution.py:54
  125.5 24.6 %all-to-all-start.5 = ((bf16[384,4,512]{2,0,1:T(8,128)(2,1)}), bf16[384,4,512]{2,0,1:T(8,128)(2,1)}, u32[]{:S(2)}, u32[]{:S(2)}) async-start(bf16[384,4,512]{2,0,1:T(8,128)(2,1)} %copy.50), calls=%async_computation.5 | async-start | bytes 3145728 | tf_op jit(solution)/shard_map/all_to_all | solution.py:55
  129.9 69.1 %all-gather.13.cloned.1.call-start = ((), (), s32[]{:S(2)}) async-start(), calls=%async_computation.9 | async-start | bytes 1474560 | tf_op jit(solution)/shard_map/all_gather | solution.py:58
  137.2 4.4 %copy-start.3 = (bf16[384,384]{1,0:T(8,128)(2,1)}, bf16[384,384]{1,0:T(8,128)(2,1)S(1)}, u32[]{:S(2)}) copy-start(bf16[384,384]{1,0:T(8,128)(2,1)S(1)} %get-tuple-element.8) | copy-start | bytes 884740
  137.2 18.4 %copy-start.4 = (bf16[384,384]{1,0:T(8,128)(2,1)}, bf16[384,384]{1,0:T(8,128)(2,1)S(1)}, u32[]{:S(2)}) copy-start(bf16[384,384]{1,0:T(8,128)(2,1)S(1)} %get-tuple-element.10) | copy-start | bytes 884740
  137.3 4.4 %copy-start.2 = (bf16[1,2048,384]{2,1,0:T(8,128)(2,1)S(1)}, bf16[1,2048,384]{2,1,0:T(8,128)(2,1)}, u32[]{:S(2)}) copy-start(bf16[1,2048,384]{2,1,0:T(8,128)(2,1)} %all-gather.9.cloned.1.call-done) | copy-start | bytes 4718596
  150.1 42.8 %all-to-all-start.3 = ((bf16[8,48,2048]{2,1,0:T(8,128)(2,1)}), bf16[8,48,2048]{2,1,0:T(8,128)(2,1)S(1)}, u32[]{:S(2)}, u32[]{:S(2)}) async-start(bf16[8,48,2048]{2,1,0:T(8,128)(2,1)} %bitcast.11), calls=%async_computation.3 | async-start | bytes 3145728 | tf_op jit(solution)/shard_map/all_to_all | solution.py:128
  155.1 47.4 %all-gather.15.cloned.1.call-start = ((), (), s32[]{:S(2)}) async-start(), calls=%async_computation.10 | async-start | bytes 1474560 | tf_op jit(solution)/shard_map/all_gather | solution.py:59
  192.9 42.1 %all-to-all-start.1 = ((bf16[8,48,2048]{2,1,0:T(8,128)(2,1)}), bf16[8,48,2048]{2,1,0:T(8,128)(2,1)}, u32[]{:S(2)}, u32[]{:S(2)}) async-start(bf16[8,48,2048]{2,1,0:T(8,128)(2,1)} %bitcast.6), calls=%async_computation.1 | async-start | bytes 3145728 | tf_op jit(solution)/shard_map/all_to_all | solution.py:105
  197.2 30.9 %all-gather.17.cloned.1.call-start = ((), (), s32[]{:S(2)}) async-start(), calls=%async_computation.11 | async-start | bytes 1474560 | tf_op jit(solution)/shard_map/all_gather | solution.py:60
  231.6 3.4 %copy-start.5 = (f32[128,2048]{1,0:T(8,128)S(1)}, f32[128,2048]{1,0:T(8,128)}, u32[]{:S(2)}) copy-start(f32[128,2048]{1,0:T(8,128)} %convert_element_type.59) | copy-start | bytes 3145732
Sparse Core Ops, SparseCore 0:
  9.8 33.5 all-gather.6
  45.3 30.8 all-gather.8
  78.0 43.4 all-gather.10
  137.4 29.3 all-gather.12
  169.0 27.5 all-gather.14
  200.1 27.9 all-gather.16
where the time goes:
time: 246 us; the launch traced here: 245 us
  waiting for transfers between devices  140 us (57%)
  matrix products  43.6 us (18%)
  starting transfers between devices  28.5 us (12%)
  local copies, waits for them, and re-layouts  17.1 us (7%)
  between operations  14.3 us (6%)
    all_to_all x1, waiting for transfers between devices, body(): lax.all_to_all(slot_grads, 'expert', split_axis=0, concat_axis=0, tiled=T...  33.6 us
    all_to_all x1, waiting for transfers between devices, body(): lax.all_to_all(send_grad, 'expert', split_axis=0, concat_axis=0, tiled=True)  30.1 us
    all_to_all x1, waiting for transfers between devices, body(): lax.all_to_all(send_rows, 'expert', split_axis=0, concat_axis=0, tiled=True)  29.9 us
    all_gather x1, waiting for transfers between devices, weight_grads(): lax.all_gather(hidden, 'dp', axis=0, tiled=True)  22.1 us
    all_to_all x1, waiting for transfers between devices, weight_grads(): lax.all_to_all(rows, 'dp', split_axis=1, concat_axis=0, tiled=True)  14.7 us
    dot_general x3, matrix products, contract_last(): lax.dot_general(left, right, (((1,), (1,)), ((), ())), preferred_element_...  12.1 us
    dot_general x3, matrix products, contract_first(): lax.dot_general(left, right, (((0,), (0,)), ((), ())), preferred_element_...  10.5 us
    all_to_all x2, local copies, waits for them, and re-layouts, weight_grads(): lax.all_to_all(rows, 'dp', split_axis=1, concat_axis=0, tiled=True)  6.92 us
  transfers between devices with their start and end apart: 12, of which 7 were waited for; matrix products, arithmetic and copies ran while one was open for 22% of the time, Pallas kernels for 0%

commit v1 on v0

--- a/solution.py
+++ b/solution.py
@@ -1,7 +1,16 @@
+import functools
+
 import jax
 import jax.numpy as jnp
 from jax import lax
+from jax.experimental import pallas as pl
+from jax.experimental.pallas import tpu as pltpu
 from jax.sharding import PartitionSpec as P
+
+BF16 = jnp.bfloat16
+F32 = jnp.float32
+CORES = 2
+VMEM_MAX = 60 * 1024 * 1024
 
 
 def slot_table(expert_ids, experts, capacity):
@@ -139,6 +148,447 @@
     return (layer_out, token_grad, route_grad, gate_grad, up_grad, down_grad)
 
 
+def pad16(n):
+    return (n + 15) // 16 * 16
+
+
+def prefix_count(member):
+    t = member.shape[1]
+    before = lax.broadcasted_iota(jnp.int32, (t, t), 0) < lax.broadcasted_iota(jnp.int32, (t, t), 1)
+    return jnp.sum(member[:, :, None] * before.astype(F32)[None], axis=1)
+
+
+def route_tables(expert_ids, route_weights, groups):
+    count, top = expert_ids.shape
+    stages = groups // CORES
+    chip = lax.axis_index("expert") // CORES
+    lanes = lax.broadcasted_iota(jnp.int32, (count,), 0)
+    experts = lax.broadcasted_iota(jnp.int32, (groups, count), 0)
+    member = jnp.zeros((groups, count), F32)
+    weight = jnp.zeros((groups, count), F32)
+    for k in range(top):
+        hit = (expert_ids[:, k][None, :] == experts).astype(F32)
+        member = member + hit
+        weight = weight + hit * route_weights[:, k][None, :]
+    slot = jnp.where(member > 0, prefix_count(member), -1.0)
+
+    def position(first):
+        key = jnp.where(first, lanes, lanes + count)
+        return jnp.sum((key[:, None] < key[None, :]).astype(F32), axis=0)
+
+    pos_up = position(jnp.any(expert_ids // CORES == stages - 1, axis=1))
+    pos_down = position(jnp.any(expert_ids // CORES == 0, axis=1))
+    dest = lax.broadcasted_iota(jnp.int32, (groups, 1), 0) // CORES
+    pos = jnp.where(dest >= chip, pos_up[None, :], pos_down[None, :])
+    pick = (pos[:, None, :] == lanes.astype(F32)[None, :, None]).astype(F32)
+    slot_rows = jnp.sum(pick * slot[:, None, :], axis=2)
+    weight_rows = jnp.sum(pick * weight[:, None, :], axis=2)
+    swap = lambda a: a.reshape(stages, CORES, count)[:, ::-1].reshape(groups, count)
+    zero = jnp.zeros_like(slot)
+    meta = jnp.stack(
+        [slot_rows, weight_rows, swap(slot_rows), slot, swap(slot), zero, zero, zero], axis=1
+    )
+    order = jnp.stack([pos_up, pos_down] + [jnp.zeros_like(pos_up)] * 6, axis=0)
+    return meta, order
+
+
+def one_hot(row, height):
+    rows = lax.broadcasted_iota(jnp.int32, (height, row.shape[1]), 0).astype(F32)
+    return (rows == row).astype(F32)
+
+
+def choose(index, values):
+    result = jnp.int32(values[0])
+    for i in range(1, len(values)):
+        result = jnp.where(index == i, jnp.int32(values[i]), result)
+    return result
+
+
+def visit_order(chip, stages):
+    near = [s for d in range(stages) for s in ((chip - d, chip + d) if d else (chip,))]
+    return [s for s in near if 0 <= s < stages]
+
+
+def moe_kernel(
+    groups, ndp, cap, edge,
+    tok_ref, grad_ref, meta_ref, order_ref, wg_ref, wu_ref, wd_ref,
+    out_ref, tgrad_ref, route_ref, gg_ref, ug_ref, dg_ref,
+    blocks, own_down, metas, xr, gr, ogr, wr, wfull, y, partner, ret_in, ret_down, ret_out,
+    grad_send, grad_own, grad_recv, route_out, route_in,
+    in_send, in_recv, meta_send, meta_recv, w_send, w_recv, pc_send, pc_recv,
+    ret_send, ret_recv, retd_recv, route_send, route_recv, gr_send, gr_recv,
+):
+    stages = groups // CORES
+    count, width = tok_ref.shape
+    part, ff = wg_ref.shape
+    me = lax.axis_index("expert")
+    dp = lax.axis_index("dp")
+    chip, core = me // CORES, me % CORES
+    mate = chip * CORES + (1 - core)
+    at_edge = (chip == 0) | (chip == stages - 1)
+    pending = []
+
+    def copy(src, dst, ssem, rsem, where):
+        return pltpu.make_async_remote_copy(
+            src_ref=src, dst_ref=dst, send_sem=ssem, recv_sem=rsem,
+            device_id=where, device_id_type=pl.DeviceIdType.MESH,
+        )
+
+    def send(cond, *args):
+        if cond is None:
+            copy(*args).start()
+        else:
+            pl.when(cond)(lambda: copy(*args).start())
+        pending.append((cond, args))
+
+    def send_rows(cond, short, src, dst, ssem, rsem, where):
+        if edge == count:
+            send(cond, src, dst, ssem, rsem, where)
+            return
+        full = jnp.logical_not(short)
+        if cond is not None:
+            short, full = cond & short, cond & full
+        cut = pl.ds(0, edge)
+        send(full, src, dst, ssem, rsem, where)
+        send(short, src.at[cut], dst.at[cut], ssem, rsem, where)
+
+    def wait_rows(cond, short, dst, sem):
+        def one(c, ref):
+            pl.when(c)(lambda: copy(ref, ref, sem, sem, {"expert": mate}).wait_recv())
+
+        if edge == count:
+            one(cond, dst)
+            return
+        one(cond & jnp.logical_not(short), dst)
+        one(cond & short, dst.at[pl.ds(0, edge)])
+
+    yes = chip >= 0
+    if edge < count:
+        rest = pl.ds(edge, count - edge)
+        empty = jnp.zeros((count - edge, width), BF16)
+        for t in range(2):
+            for s in range(stages):
+                blocks[0, t, s, rest] = empty
+                blocks[1, t, s, rest] = empty
+                ret_in[t, s, rest] = empty
+            ret_down[t, rest] = empty
+    for t in range(2):
+        @pl.when(chip == stages - 1)
+        def _():
+            ret_in[t, chip] = jnp.zeros((count, width), BF16)
+
+        @pl.when(chip == 0)
+        def _():
+            ret_down[t] = jnp.zeros((count, width), BF16)
+
+    up_hot = one_hot(order_ref[0:1, :], count)
+    down_hot = one_hot(order_ref[1:2, :], count)
+    for t, ref in enumerate((tok_ref, grad_ref)):
+        value = ref[...]
+        blocks[0, t, chip] = jnp.dot(up_hot.astype(BF16), value, preferred_element_type=F32).astype(BF16)
+        own_down[t] = jnp.dot(down_hot.astype(BF16), value, preferred_element_type=F32).astype(BF16)
+    metas[me] = meta_ref[me]
+
+    barrier = pltpu.get_barrier_semaphore()
+    for off in range(1, groups):
+        pl.semaphore_signal(barrier, inc=1, device_id={"expert": (me + off) % groups},
+                            device_id_type=pl.DeviceIdType.MESH)
+    for off in range(1, ndp):
+        pl.semaphore_signal(barrier, inc=1, device_id={"dp": (dp + off) % ndp},
+                            device_id_type=pl.DeviceIdType.MESH)
+    pl.semaphore_wait(barrier, groups + ndp - 2)
+
+    for off in range(1, groups):
+        other = (me + off) % groups
+        send(None, meta_ref.at[other], metas.at[me], meta_send.at[off - 1], meta_recv.at[off - 1],
+             {"expert": other})
+    has_up, has_down = chip < stages - 1, chip > 0
+    up_dev, down_dev = {"expert": me + CORES}, {"expert": me - CORES}
+    for t in range(2):
+        send_rows(has_up, chip + 1 == stages - 1, blocks.at[0, t, chip], blocks.at[0, t, chip],
+                  in_send.at[t, 0, 0], in_recv.at[0, t, chip], up_dev)
+        send_rows(has_down, chip - 1 == 0, own_down.at[t], blocks.at[0, t, chip],
+                  in_send.at[t, 0, 1], in_recv.at[0, t, chip], down_dev)
+        send(None, blocks.at[0, t, chip], blocks.at[1, t, chip],
+             in_send.at[t, 0, 2], in_recv.at[1, t, chip], {"expert": mate})
+    for i, ref in enumerate((wg_ref, wu_ref, wd_ref)):
+        for off in range(1, ndp):
+            send(None, ref, wfull.at[i, dp], w_send.at[i, off - 1], w_recv.at[i, off - 1],
+                 {"dp": (dp + off) % ndp})
+        wfull[i, dp] = ref[...]
+    for off in range(1, groups):
+        copy(meta_ref.at[0], metas.at[0], meta_send.at[off - 1], meta_recv.at[off - 1],
+             {"expert": mate}).wait_recv()
+
+    table = [visit_order(z, stages) for z in range(stages)]
+    source = [choose(chip, [table[z][q] for z in range(stages)]) for q in range(stages)]
+
+    def compact(q, r):
+        s = source[q]
+        origin = s * CORES + (core if r == 0 else 1 - core)
+        tile = metas[origin]
+        hot = one_hot(tile[0:1, :], cap)
+        scale = jnp.sum(hot * tile[1:2, :], axis=1, keepdims=True)
+        hot = hot.astype(BF16)
+        rows = pl.ds((q * 2 + r) * cap, cap)
+        xr[rows, :] = jnp.dot(hot, blocks[r, 0, s], preferred_element_type=F32).astype(BF16)
+        g = jnp.dot(hot, blocks[r, 1, s], preferred_element_type=F32)
+        gr[rows, :] = g.astype(BF16)
+        ogr[rows, :] = (scale * g).astype(BF16)
+        wr[rows, :] = jnp.broadcast_to(scale, (cap, 128))
+
+    compact(0, 0)
+    for q in range(stages):
+        s = source[q]
+        if q:
+            rising = s < chip
+            nxt = jnp.where(rising, chip + 1, chip - 1)
+            more = (nxt >= 0) & (nxt < stages)
+            for t in range(2):
+                wait_rows(yes, at_edge, blocks.at[0, t, s], in_recv.at[0, t, s])
+                send_rows(more, (nxt == 0) | (nxt == stages - 1), blocks.at[0, t, s],
+                          blocks.at[0, t, s], in_send.at[t, q, 0], in_recv.at[0, t, s],
+                          {"expert": nxt * CORES + core})
+                send_rows(None, at_edge, blocks.at[0, t, s], blocks.at[1, t, s],
+                          in_send.at[t, q, 2], in_recv.at[1, t, s], {"expert": mate})
+            compact(q, 0)
+        for t in range(2):
+            if q:
+                wait_rows(yes, at_edge, blocks.at[1, t, s], in_recv.at[1, t, s])
+            else:
+                wait_rows(yes, chip < 0, blocks.at[1, t, s], in_recv.at[1, t, s])
+        compact(q, 1)
+
+    for i in range(3):
+        for off in range(1, ndp):
+            copy(wfull.at[i, 0], wfull.at[i, 0], w_send.at[i, 0], w_recv.at[i, off - 1],
+                 {"expert": mate}).wait_recv()
+
+    def nt(a, b):
+        return lax.dot_general(a, b, (((1,), (1,)), ((), ())), preferred_element_type=F32)
+
+    def tn(a, b):
+        return lax.dot_general(a, b, (((0,), (0,)), ((), ())), preferred_element_type=F32)
+
+    def cut(j):
+        return pl.ds(j * part, part)
+
+    total = xr.shape[0]
+    gate = jnp.zeros((total, ff), F32)
+    up = jnp.zeros((total, ff), F32)
+    hg = jnp.zeros((total, ff), F32)
+    for j in range(ndp):
+        gate += jnp.dot(xr[:, cut(j)], wfull[0, j], preferred_element_type=F32)
+        up += jnp.dot(xr[:, cut(j)], wfull[1, j], preferred_element_type=F32)
+        hg += jnp.dot(ogr[:, cut(j)], wfull[2, j], preferred_element_type=F32)
+    sig = jax.nn.sigmoid(gate)
+    hidden = (gate * sig * up).astype(BF16)
+    gt = (hg * up * sig * (1.0 + gate * (1.0 - sig))).astype(BF16)
+    ut = (hg * gate * sig).astype(BF16)
+    scale = wr[:, 0:1]
+    dots = jnp.zeros((total, 1), F32)
+    for j in range(ndp):
+        eo = nt(hidden, wfull[2, j]).astype(BF16).astype(F32)
+        y[0, :, cut(j)] = (scale * eo).astype(BF16)
+        dots += jnp.sum(gr[:, cut(j)].astype(F32) * eo, axis=1, keepdims=True)
+        y[1, :, cut(j)] = (nt(gt, wfull[0, j]) + nt(ut, wfull[1, j])).astype(BF16)
+
+    for q in reversed(range(stages)):
+        for t in range(2):
+            send(None, y.at[t, pl.ds((q * 2 + 1) * cap, cap)], partner.at[t, q],
+                 pc_send.at[t, q], pc_recv.at[t, q], {"expert": mate})
+
+    both = jnp.concatenate([gt, ut], axis=1)
+
+    def weight_slice(off):
+        j = (dp + off) % ndp
+        cols = pl.ds(pl.multiple_of(j * part, part), part)
+        gu = tn(xr[:, cols], both)
+        return gu[:, :ff], gu[:, ff:], tn(ogr[:, cols], hidden)
+
+    def weight_part(off):
+        for i, value in enumerate(weight_slice(off)):
+            grad_send[i, off - 1] = value.astype(BF16)
+        for i in range(3):
+            send(None, grad_send.at[i, off - 1], grad_recv.at[i, off - 1], gr_send.at[i, off - 1],
+                 gr_recv.at[i, off - 1], {"dp": (dp + off) % ndp})
+
+    def expand(q, t, row_own, row_mate):
+        tile = metas[source[q] * CORES + core]
+        own = one_hot(tile[row_own:row_own + 1, :], cap).astype(BF16)
+        other = one_hot(tile[row_mate:row_mate + 1, :], cap).astype(BF16)
+        return tn(own, y[t, pl.ds(q * 2 * cap, cap), :]) + tn(other, partner[t, q])
+
+    def give_back(q):
+        s = source[q]
+        rising = s > chip
+        nxt = jnp.where(rising, chip + 1, chip - 1)
+        back = jnp.where(rising, chip - 1, chip + 1)
+        fed = (back >= 0) & (back < stages)
+        where = {"expert": nxt * CORES + core}
+        for t in range(2):
+            copy(partner.at[t, q], partner.at[t, q], pc_send.at[t, q], pc_recv.at[t, q],
+                 {"expert": mate}).wait_recv()
+            value = expand(q, t, 0, 2)
+            wait_rows(fed, (back == 0) | (back == stages - 1), ret_in.at[t, s], ret_recv.at[t, s])
+
+            @pl.when(fed)
+            def _():
+                ret_out[t, q] = (value + ret_in[t, s].astype(F32)).astype(BF16)
+
+            @pl.when(jnp.logical_not(fed))
+            def _():
+                ret_out[t, q] = value.astype(BF16)
+
+            last_up = rising & (nxt == s)
+            send_rows(last_up, at_edge, ret_out.at[t, q], ret_down.at[t], ret_send.at[t, q],
+                      retd_recv.at[t], where)
+            send_rows(jnp.logical_not(last_up), at_edge, ret_out.at[t, q], ret_in.at[t, s],
+                      ret_send.at[t, q], ret_recv.at[t, s], where)
+
+    for off in range(1, ndp):
+        q = stages - off
+        if q >= 1:
+            give_back(q)
+        weight_part(off)
+    for q in reversed(range(1, stages - ndp + 1)):
+        give_back(q)
+
+    for q in range(stages):
+        for r in range(2):
+            origin = source[q] * CORES + (core if r == 0 else 1 - core)
+            hot = one_hot(metas[origin][3:4, :], cap)
+            part_dots = dots[(q * 2 + r) * cap:(q * 2 + r + 1) * cap, :]
+            line = jnp.sum(hot * part_dots, axis=0, keepdims=True)
+            route_out[origin] = jnp.broadcast_to(line, (8, count))
+    for off in range(1, groups):
+        other = (me + off) % groups
+        send(None, route_out.at[other], route_in.at[me], route_send.at[off - 1],
+             route_recv.at[off - 1], {"expert": other})
+    route_in[me] = route_out[me]
+
+    own = weight_slice(0)
+    for i in range(3):
+        grad_own[i] = own[i]
+
+    for t, ref in enumerate((out_ref, tgrad_ref)):
+        copy(partner.at[t, 0], partner.at[t, 0], pc_send.at[t, 0], pc_recv.at[t, 0],
+             {"expert": mate}).wait_recv()
+        value = expand(0, t, 3, 4)
+        wait_rows(has_up, chip + 1 == stages - 1, ret_in.at[t, chip], ret_recv.at[t, chip])
+        wait_rows(has_down, chip - 1 == 0, ret_down.at[t], retd_recv.at[t])
+        value += tn(up_hot.astype(BF16), ret_in[t, chip]) + tn(down_hot.astype(BF16), ret_down[t])
+        ref[...] = value.astype(BF16)
+
+    for off in range(1, groups):
+        copy(route_out.at[0], route_in.at[0], route_send.at[off - 1], route_recv.at[off - 1],
+             {"expert": mate}).wait_recv()
+    route_ref[...] = route_in[...]
+    for i, ref in enumerate((gg_ref, ug_ref, dg_ref)):
+        value = grad_own[i]
+        for off in range(1, ndp):
+            copy(grad_recv.at[i, off - 1], grad_recv.at[i, off - 1], gr_send.at[i, off - 1],
+                 gr_recv.at[i, off - 1], {"expert": mate}).wait_recv()
+            value += grad_recv[i, off - 1].astype(F32)
+        ref[...] = value.astype(BF16)
+    for cond, args in pending:
+        if cond is None:
+            copy(*args).wait_send()
+        else:
+            pl.when(cond)(lambda args=args: copy(*args).wait_send())
+
+
+def kernel_scratch(groups, ndp, cap, count, width, part, ff):
+    stages = groups // CORES
+    rows = groups * cap
+    shapes = [
+        ((2, 2, stages, count, width), BF16),
+        ((2, count, width), BF16),
+        ((groups, 8, count), F32),
+        ((rows, width), BF16),
+        ((rows, width), BF16),
+        ((rows, width), BF16),
+        ((rows, 128), F32),
+        ((3, ndp, part, ff), BF16),
+        ((2, rows, width), BF16),
+        ((2, stages, cap, width), BF16),
+        ((2, stages, count, width), BF16),
+        ((2, count, width), BF16),
+        ((2, stages, count, width), BF16),
+        ((3, ndp - 1, part, ff), BF16),
+        ((3, part, ff), F32),
+        ((3, ndp - 1, part, ff), BF16),
+        ((groups, 8, count), F32),
+        ((groups, 8, count), F32),
+    ]
+    sems = [
+        (2, stages, 3), (2, 2, stages), (groups - 1,), (groups - 1,), (3, ndp - 1), (3, ndp - 1),
+        (2, stages), (2, stages), (2, stages), (2, stages), (2,), (groups - 1,), (groups - 1,),
+        (3, ndp - 1), (3, ndp - 1),
+    ]
+    return shapes, sems
+
+
+def scratch_bytes(shapes):
+    total = 0
+    for shape, dtype in shapes:
+        size = jnp.dtype(dtype).itemsize
+        for n in shape:
+            size *= n
+        total += size
+    return total
+
+
+def slot_capacity(count, top, experts):
+    return max(2, (3 * count * top + 2 * experts - 1) // (2 * experts))
+
+
+def line_body(groups, ndp, tokens, expert_ids, route_weights, w_gate, w_up, w_down, grad_out):
+    count, width = tokens.shape
+    _, part, ff = w_gate.shape
+    top = expert_ids.shape[1]
+    slots = slot_capacity(count, top, groups)
+    cap = pad16(slots)
+    edge = min(count, pad16(CORES * slots))
+    meta, order = route_tables(expert_ids, route_weights, groups)
+    shapes, sems = kernel_scratch(groups, ndp, cap, count, width, part, ff)
+    vmem = pl.BlockSpec(memory_space=pltpu.VMEM)
+    layer_out, token_grad, route, gate_g, up_g, down_g = pl.pallas_call(
+        functools.partial(moe_kernel, groups, ndp, cap, edge),
+        out_shape=(
+            jax.ShapeDtypeStruct((count, width), BF16),
+            jax.ShapeDtypeStruct((count, width), BF16),
+            jax.ShapeDtypeStruct((groups, 8, count), F32),
+            jax.ShapeDtypeStruct((part, ff), BF16),
+            jax.ShapeDtypeStruct((part, ff), BF16),
+            jax.ShapeDtypeStruct((part, ff), BF16),
+        ),
+        in_specs=[vmem] * 7,
+        out_specs=(vmem,) * 6,
+        scratch_shapes=[pltpu.VMEM(s, d) for s, d in shapes]
+        + [pltpu.SemaphoreType.DMA(s) for s in sems],
+        compiler_params=pltpu.CompilerParams(
+            collective_id=0, has_side_effects=True, vmem_limit_bytes=VMEM_MAX
+        ),
+    )(tokens, grad_out, meta, order, w_gate[0], w_up[0], w_down[0])
+    experts = lax.broadcasted_iota(jnp.int32, (groups, count, top), 0)
+    mine = (expert_ids[None] == experts).astype(F32)
+    route_grad = jnp.sum(mine * route[:, 0, :, None], axis=0)
+    return layer_out, token_grad, route_grad, gate_g[None], up_g[None], down_g[None]
+
+
+def pick_body(groups, ndp, *args):
+    tokens, expert_ids, _, w_gate = args[:4]
+    count, width = tokens.shape
+    local, part, ff = w_gate.shape
+    if local == 1 and groups % CORES == 0 and groups > CORES and ndp > 1:
+        cap = pad16(slot_capacity(count, expert_ids.shape[1], groups))
+        shapes, _ = kernel_scratch(groups, ndp, cap, count, width, part, ff)
+        if scratch_bytes(shapes) < VMEM_MAX * 3 // 4:
+            return line_body(groups, ndp, *args)
+    return body(*args)
+
+
 def solution(mesh):
     in_specs = (
         P(("dp", "expert"), None),
@@ -157,4 +607,5 @@
         P("expert", "dp", None),
         P("expert", "dp", None),
     )
-    return jax.shard_map(body, mesh=mesh, in_specs=in_specs, out_specs=out_specs, check_vma=False)
+    step = functools.partial(pick_body, mesh.shape["expert"], mesh.shape["dp"])
+    return jax.shard_map(step, mesh=mesh, in_specs=in_specs, out_specs=out_specs, check_vma=False)

time: 246 us -> 181 us (0.74)
  the two profiles are of different devices: /device:TPU:0 before, /device:TPU:10 now
where the time goes in v1:
time: 181 us
  Pallas kernels  169 us (93%)
  local copies, waits for them, and re-layouts  9.15 us (5%)
  other arithmetic  2.32 us (1%)
    pallas_call x1, Pallas kernels, line_body(): pl.pallas_call(functools.partial(moe_kernel, groups, ndp, cap, edge), out...  169 us
    unnamed x17, local copies, waits for them, and re-layouts  7.5 us

profile of v1, /device:TPU:10, one launch (start us, length us, event | category | flops | bytes accessed | tf_op | source)
XLA Modules:
  0.0 180.8 jit_solution(91633653393076470)
XLA Ops:
  0.7 0.1 pad.2.clone
  0.7 0.1 pad.3.clone
  0.8 0.0 copy-start.5
  0.8 0.7 copy-done.5
  1.5 0.0 copy-start.4
  1.5 0.7 copy-done.4
  2.2 0.1 convert_reduce_fusion
  2.3 0.1 convert_reduce_fusion.1
  2.4 0.7 maximum_maximum_fusion.order_ref
  3.1 0.1 broadcast_select_fusion
  3.2 0.2 multiply_reduce_fusion
  3.4 0.1 compare_select_fusion.3
  3.5 0.4 fusion.1
  4.0 0.7 stack.27.meta_ref
  4.7 168.6 %shard_map.118 = (bf16[128,2048]{1,0:T(8,128)(2,1)}, bf16[128,2048]{1,0:T(8,128)(2,1)}, f32[8,8,128]{2,1,0:T(8,128)}, bf16[512,384]{1,0:T(8,128)(2,1)}, bf16[512...) custom-call(bf16[128,2048]{1,0:T(8,128)(2,1)} %tok_ref.1, bf16[128,2048]{1,0:T(8,128)(2,1)} %grad_ref.1, ...), custom_call_target="tpu_custom_call" | custom-call | tf_op jit(solution)/shard_map/pallas_call | solution.py:556
  173.3 0.8 slice.19
  174.1 0.6 select_reduce_fusion
  174.7 0.0 copy-start
  174.7 1.9 %copy.19 = bf16[128,2048]{1,0:T(8,128)(2,1)} copy(bf16[128,2048]{1,0:T(8,128)(2,1)} %get-tuple-element.36) | data formatting | bytes 1048576
  176.6 0.0 copy-done
  176.6 0.0 copy-start.3
  176.6 0.8 copy.20
  177.4 0.4 copy-done.3
  177.8 0.0 copy-start.2
  177.8 0.7 copy.21
  178.5 0.4 copy-done.2
  178.9 0.0 copy-start.1
  178.9 0.7 copy.22
  179.7 0.4 copy-done.1
  180.1 0.7 copy.23
  (17 shorter events, 0.2 us)
Async XLA Ops:
  0.8 0.7 copy-start.5
  1.5 0.7 copy-start.4
  174.7 1.9 %copy-start = (bf16[128,2048]{1,0:T(8,128)(2,1)S(1)}, bf16[128,2048]{1,0:T(8,128)(2,1)}, u32[]{:S(2)}) copy-start(bf16[128,2048]{1,0:T(8,128)(2,1)} %get-tuple-element.37) | copy-start | bytes 1572868
  176.6 1.2 copy-start.3
  177.8 1.1 copy-start.2
  178.9 1.1 copy-start.1

commit v2 on v1

--- a/solution.py
+++ b/solution.py
@@ -387,16 +387,19 @@
     ut = (hg * gate * sig).astype(BF16)
     scale = wr[:, 0:1]
     dots = jnp.zeros((total, 1), F32)
+    def to_mate(t):
+        for q in reversed(range(stages)):
+            send(None, y.at[t, pl.ds((q * 2 + 1) * cap, cap)], partner.at[t, q],
+                 pc_send.at[t, q], pc_recv.at[t, q], {"expert": mate})
+
     for j in range(ndp):
         eo = nt(hidden, wfull[2, j]).astype(BF16).astype(F32)
         y[0, :, cut(j)] = (scale * eo).astype(BF16)
         dots += jnp.sum(gr[:, cut(j)].astype(F32) * eo, axis=1, keepdims=True)
+    to_mate(0)
+    for j in range(ndp):
         y[1, :, cut(j)] = (nt(gt, wfull[0, j]) + nt(ut, wfull[1, j])).astype(BF16)
-
-    for q in reversed(range(stages)):
-        for t in range(2):
-            send(None, y.at[t, pl.ds((q * 2 + 1) * cap, cap)], partner.at[t, q],
-                 pc_send.at[t, q], pc_recv.at[t, q], {"expert": mate})
+    to_mate(1)
 
     both = jnp.concatenate([gt, ut], axis=1)
 
@@ -419,40 +422,41 @@
         other = one_hot(tile[row_mate:row_mate + 1, :], cap).astype(BF16)
         return tn(own, y[t, pl.ds(q * 2 * cap, cap), :]) + tn(other, partner[t, q])
 
-    def give_back(q):
+    def give_back(q, ends):
         s = source[q]
         rising = s > chip
         nxt = jnp.where(rising, chip + 1, chip - 1)
         back = jnp.where(rising, chip - 1, chip + 1)
-        fed = (back >= 0) & (back < stages)
         where = {"expert": nxt * CORES + core}
+        here = at_edge if ends else jnp.logical_not(at_edge)
         for t in range(2):
-            copy(partner.at[t, q], partner.at[t, q], pc_send.at[t, q], pc_recv.at[t, q],
-                 {"expert": mate}).wait_recv()
-            value = expand(q, t, 0, 2)
-            wait_rows(fed, (back == 0) | (back == stages - 1), ret_in.at[t, s], ret_recv.at[t, s])
-
-            @pl.when(fed)
+            pl.when(here)(lambda t=t: copy(
+                partner.at[t, q], partner.at[t, q], pc_send.at[t, q], pc_recv.at[t, q],
+                {"expert": mate}).wait_recv())
+            if not ends:
+                wait_rows(here, (back == 0) | (back == stages - 1), ret_in.at[t, s],
+                          ret_recv.at[t, s])
+
+            @pl.when(here)
             def _():
-                ret_out[t, q] = (value + ret_in[t, s].astype(F32)).astype(BF16)
-
-            @pl.when(jnp.logical_not(fed))
-            def _():
+                value = expand(q, t, 0, 2)
+                if not ends:
+                    value = value + ret_in[t, s].astype(F32)
                 ret_out[t, q] = value.astype(BF16)
 
-            last_up = rising & (nxt == s)
-            send_rows(last_up, at_edge, ret_out.at[t, q], ret_down.at[t], ret_send.at[t, q],
-                      retd_recv.at[t], where)
-            send_rows(jnp.logical_not(last_up), at_edge, ret_out.at[t, q], ret_in.at[t, s],
-                      ret_send.at[t, q], ret_recv.at[t, s], where)
-
+            arrives = rising & (nxt == s)
+            rows = pl.ds(0, edge) if ends else pl.ds(0, count)
+            send(here & arrives, ret_out.at[t, q, rows], ret_down.at[t, rows], ret_send.at[t, q],
+                 retd_recv.at[t], where)
+            send(here & jnp.logical_not(arrives), ret_out.at[t, q, rows], ret_in.at[t, s, rows],
+                 ret_send.at[t, q], ret_recv.at[t, s], where)
+
+    for q in reversed(range(1, stages)):
+        give_back(q, True)
     for off in range(1, ndp):
-        q = stages - off
-        if q >= 1:
-            give_back(q)
         weight_part(off)
-    for q in reversed(range(1, stages - ndp + 1)):
-        give_back(q)
+    for q in reversed(range(1, stages)):
+        give_back(q, False)
 
     for q in range(stages):
         for r in range(2):

time: 181 us -> 156 us (0.86)
  the two profiles are of different devices: /device:TPU:10 before, /device:TPU:0 now
where the time goes in v2:
time: 156 us
  Pallas kernels  143 us (92%)
  local copies, waits for them, and re-layouts  9.15 us (6%)
  other arithmetic  2.32 us (1%)
    pallas_call x1, Pallas kernels, line_body(): pl.pallas_call(functools.partial(moe_kernel, groups, ndp, cap, edge), out...  143 us
    unnamed x17, local copies, waits for them, and re-layouts  7.5 us

profile of v2, /device:TPU:0, one launch (start us, length us, event | category | flops | bytes accessed | tf_op | source)
XLA Modules:
  0.0 155.6 jit_solution(12571362085017857453)
XLA Ops:
  0.7 0.1 pad.2.clone
  0.7 0.1 pad.3.clone
  0.8 0.0 copy-start.5
  0.8 0.7 copy-done.5
  1.5 0.0 copy-start.4
  1.5 0.7 copy-done.4
  2.2 0.1 convert_reduce_fusion
  2.3 0.1 convert_reduce_fusion.1
  2.4 0.7 maximum_maximum_fusion.order_ref
  3.1 0.1 broadcast_select_fusion
  3.2 0.2 multiply_reduce_fusion
  3.4 0.1 compare_select_fusion.3
  3.5 0.4 fusion.1
  4.0 0.7 stack.27.meta_ref
  4.7 143.4 %shard_map.118 = (bf16[128,2048]{1,0:T(8,128)(2,1)}, bf16[128,2048]{1,0:T(8,128)(2,1)}, f32[8,8,128]{2,1,0:T(8,128)}, bf16[512,384]{1,0:T(8,128)(2,1)}, bf16[512...) custom-call(bf16[128,2048]{1,0:T(8,128)(2,1)} %tok_ref.1, bf16[128,2048]{1,0:T(8,128)(2,1)} %grad_ref.1, ...), custom_call_target="tpu_custom_call" | custom-call | tf_op jit(solution)/shard_map/pallas_call | solution.py:560
  148.1 0.8 slice.19
  148.8 0.6 select_reduce_fusion
  149.4 0.0 copy-start
  149.4 1.9 %copy.19 = bf16[128,2048]{1,0:T(8,128)(2,1)} copy(bf16[128,2048]{1,0:T(8,128)(2,1)} %get-tuple-element.36) | data formatting | bytes 1048576
  151.3 0.0 copy-done
  151.4 0.0 copy-start.3
  151.4 0.8 copy.20
  152.1 0.4 copy-done.3
  152.5 0.0 copy-start.2
  152.5 0.7 copy.21
  153.3 0.4 copy-done.2
  153.7 0.0 copy-start.1
  153.7 0.7 copy.22
  154.4 0.4 copy-done.1
  154.8 0.7 copy.23
  (17 shorter events, 0.2 us)
Async XLA Ops:
  0.8 0.7 copy-start.5
  1.5 0.7 copy-start.4
  149.4 1.9 %copy-start = (bf16[128,2048]{1,0:T(8,128)(2,1)S(1)}, bf16[128,2048]{1,0:T(8,128)(2,1)}, u32[]{:S(2)}) copy-start(bf16[128,2048]{1,0:T(8,128)(2,1)} %get-tuple-element.37) | copy-start | bytes 1572868
  151.4 1.2 copy-start.3
  152.5 1.1 copy-start.2
  153.7 1.1 copy-start.1
